TPU v7x, 32 devices: a whole 2x2x4 slice. The times are simulated.
32 devices in a mesh: seq: 4 (over y, x), exp: 8 (over z, core).
Axes of the slice: x: 2, y: 2, z: 4, core: 2. Of those that a mesh axis runs over, the one named last changes fastest.
Arguments:
- queries: bfloat16 [4096, 3072], P(('seq', 'exp')), may hold values from -123 to 123
- keys: bfloat16 [4096, 512], P(('seq', 'exp')), may hold values from -6 to 6
- values: bfloat16 [4096, 512], P(('seq', 'exp')), may hold values from -9 to 9
- residual: bfloat16 [4096, 6144], P(('seq', 'exp')), may hold values from -51 to 51
- proj_weight: bfloat16 [3072, 6144], P('seq', 'exp'), may hold values from -0.109375 to 0.109375
- norm_gain: bfloat16 [6144], replicated, may hold values from 0.099609375 to 1.8984375
- router: bfloat16 [6144, 8], replicated, may hold values from -0.078125 to 0.078125
- expert_ids: int32 [4096, 2], P(('seq', 'exp')), may hold values from 0 to 7, all different within a row; in each aligned block of 128 rows (0 to 127, 128 to 255, ...) at most 33 rows name the same one
- u_gate_up: bfloat16 [8, 6144, 1024], P('exp'), may hold values from -0.078125 to 0.078125
- v_gate_up: bfloat16 [8, 2, 512, 8192], P('exp'), may hold values from -0.25 to 0.25
- u_down: bfloat16 [8, 8192, 512], P('exp'), may hold values from -0.0625 to 0.0625
- v_down: bfloat16 [8, 512, 6144], P('exp'), may hold values from -0.25 to 0.25
Outputs:
- layer_out: bfloat16 [4096, 6144], P(('seq', 'exp'))
Inputs may be any that keep to these rules, and one draw needn't show every extreme that they name: `expert_ids`: the two experts of a token differ. Among the tokens of one device no expert is named more than 33 times, and in some devices' tokens some expert is named exactly 33 times.
All inputs are finite; a program needn't handle non-finite values.
Results may differ from a plain program's by a relative error of at most 0.02.
Values may be sent and summed in bfloat16 or wider, within the bound.
A program may use at most 192 MiB of HBM per device.

v0:
```python
import jax
import jax.numpy as jnp
from jax import lax
from jax.sharding import PartitionSpec as P

D = 6144
HEADS = 24
KV_HEADS = 4
HEAD_DIM = 128
GROUP_HEADS = 3
EXPERTS = 8
RANK = 512
TOK_DEV = 128
CAP = 33
EPS = 1e-05


def swapped(x, axis, distance):
    return lax.ppermute(x, axis, [(i, i ^ 1 << distance) for i in range(lax.axis_size(axis))])


def passed_along(value, axis, steps):
    count = lax.axis_size(axis)
    pairs = [(source, (source + steps) % count) for source in range(count)]
    return lax.ppermute(value, axis, pairs)


def attend(current, query_rows, key_rows, value_rows, allowed):
    row_max, row_sum, weighted = current
    scores = jnp.einsum("qhd,kd->qhk", query_rows, key_rows, preferred_element_type=jnp.float32)
    scores = scores * HEAD_DIM ** (-0.5)
    if allowed is not None:
        scores = jnp.where(allowed[:, None, :], scores, -jnp.inf)
    new_max = jnp.maximum(row_max, jnp.max(scores, axis=-1))
    fading = jnp.exp(row_max - new_max)
    exp_terms = jnp.exp(scores - new_max[..., None])
    row_sum = row_sum * fading + jnp.sum(exp_terms, axis=-1)
    update = jnp.einsum(
        "qhk,kd->qhd",
        exp_terms.astype(jnp.bfloat16),
        value_rows,
        preferred_element_type=jnp.float32,
    )
    weighted = weighted * fading[..., None] + update
    return (new_max, row_sum, weighted)


def fresh_states(count_rows):
    query_step = min(512, count_rows)
    states = [
        (
            jnp.full((query_step, GROUP_HEADS), -1e30, jnp.float32),
            jnp.zeros((query_step, GROUP_HEADS), jnp.float32),
            jnp.zeros((query_step, GROUP_HEADS, HEAD_DIM), jnp.float32),
        )
    ]
    return states


def attend_all(states, query_rows, query_pos, key_rows, value_rows, key_pos, mode):
    current = states[0]
    if mode == "open":
        current = attend(current, query_rows, key_rows, value_rows, None)
    else:
        allowed = key_pos[None, :] <= query_pos[:, None]
        current = attend(current, query_rows, key_rows, value_rows, allowed)
    updated = [current]
    return updated


def pick_states(stacked, which):
    return [
        tuple((lax.dynamic_index_in_dim(member, which, 0, keepdims=False) for member in tile))
        for tile in stacked
    ]


def put_states(stacked, which, fresh):
    return [
        tuple(
            (
                lax.dynamic_update_index_in_dim(member, newer, which, 0)
                for member, newer in zip(tile, new_tile)
            )
        )
        for tile, new_tile in zip(stacked, fresh)
    ]


def finish(states):
    results = [weighted / row_sum[..., None] for row_max, row_sum, weighted in states]
    joined = results[0].astype(jnp.bfloat16)
    return joined.reshape(joined.shape[0], GROUP_HEADS * HEAD_DIM)


def per_device(
    queries,
    keys,
    values,
    residual,
    proj_weight,
    norm_gain,
    router,
    expert_ids,
    u_gate_up,
    v_gate_up,
    u_down,
    v_down,
):
    seq_count = lax.axis_size("seq")
    exp_count = lax.axis_size("exp")
    seq_index = lax.axis_index("seq")
    exp_index = lax.axis_index("exp")
    group_count = HEADS // GROUP_HEADS
    split_count = exp_count // group_count
    group_width = GROUP_HEADS * HEAD_DIM
    token_rows = TOK_DEV // split_count
    block_len = TOK_DEV * exp_count
    query_count = exp_count * token_rows
    per_kv = group_count // KV_HEADS
    half_index = exp_index // group_count
    query_send = queries.reshape(token_rows, exp_count, group_width)
    kv_shape = (TOK_DEV, split_count, KV_HEADS, per_kv, HEAD_DIM)
    key_send = jnp.broadcast_to(keys.reshape(TOK_DEV, 1, KV_HEADS, 1, HEAD_DIM), kv_shape).reshape(
        TOK_DEV, exp_count, HEAD_DIM
    )
    value_send = jnp.broadcast_to(
        values.reshape(TOK_DEV, 1, KV_HEADS, 1, HEAD_DIM), kv_shape
    ).reshape(TOK_DEV, exp_count, HEAD_DIM)
    query_got, key_got, value_got = (
        lax.all_to_all(query_send, "exp", split_axis=1, concat_axis=0, tiled=True),
        lax.all_to_all(key_send, "exp", split_axis=1, concat_axis=0, tiled=True),
        lax.all_to_all(value_send, "exp", split_axis=1, concat_axis=0, tiled=True),
    )
    query_local = query_got.reshape(query_count, GROUP_HEADS, HEAD_DIM)
    key_local = key_got.reshape(block_len, HEAD_DIM)
    value_local = value_got.reshape(block_len, HEAD_DIM)
    row_ids = jnp.arange(query_count, dtype=jnp.int32)
    in_block = row_ids // token_rows * TOK_DEV + row_ids % token_rows * split_count + half_index
    key_offsets = jnp.arange(block_len, dtype=jnp.int32)
    half_q = query_count // 2
    half_k = block_len // 2
    query_near = query_local[:half_q]
    query_far = query_local[half_q:]
    key_far = key_local[half_k:]
    value_far = value_local[half_k:]
    for bit_index in range(seq_count.bit_length() - 1):
        query_far, key_far, value_far = swapped((query_far, key_far, value_far), "seq", bit_index)
    mirror_index = seq_count - 1 - seq_index
    near_pos = seq_index * block_len + in_block[:half_q]
    far_pos = mirror_index * block_len + in_block[half_q:]
    query_pair = jnp.stack([query_near, query_far])
    pair_states = [
        tuple((jnp.stack([member, member]) for member in tile)) for tile in fresh_states(half_q)
    ]
    held_blocks = (key_local[:half_k], value_local[:half_k], key_far, value_far)
    for step_index in range(seq_count):
        if step_index + 1 < seq_count:
            arrived = passed_along(
                (held_blocks[0], held_blocks[1], held_blocks[2], held_blocks[3]), "seq", 1
            )
        source = (seq_index - step_index) % seq_count
        low_keys, low_values, high_keys, high_values = held_blocks
        if step_index == 0:
            low_pos = source * block_len + key_offsets[:half_k]
            high_pos = (seq_count - 1 - source) * block_len + half_k + key_offsets[:half_k]
            near_now = pick_states(pair_states, 0)
            near_now = attend_all(
                near_now, query_near, near_pos, low_keys, low_values, low_pos, "masked"
            )
            pair_states = put_states(pair_states, 0, near_now)
            far_now = pick_states(pair_states, 1)
            far_now = attend_all(
                far_now, query_far, far_pos, high_keys, high_values, high_pos, "masked"
            )
            pair_states = put_states(pair_states, 1, far_now)
        else:
            first_low = source <= seq_index
            first_slot = jnp.where(first_low, 0, 1).astype(jnp.int32)
            key_pick = jnp.where(first_low, low_keys, high_keys)
            value_pick = jnp.where(first_low, low_values, high_values)
            query_pick = lax.dynamic_index_in_dim(query_pair, first_slot, 0, keepdims=False)
            picked_states = attend_all(
                pick_states(pair_states, first_slot),
                query_pick,
                None,
                key_pick,
                value_pick,
                None,
                "open",
            )
            pair_states = put_states(pair_states, first_slot, picked_states)
        second_high = source >= seq_count - seq_index
        second_slot = jnp.where(second_high, 0, 1).astype(jnp.int32)
        key_pick = jnp.where(second_high, high_keys, low_keys)
        value_pick = jnp.where(second_high, high_values, low_values)
        query_pick = lax.dynamic_index_in_dim(query_pair, second_slot, 0, keepdims=False)
        picked_states = attend_all(
            pick_states(pair_states, second_slot),
            query_pick,
            None,
            key_pick,
            value_pick,
            None,
            "open",
        )
        pair_states = put_states(pair_states, second_slot, picked_states)
        if step_index + 1 < seq_count:
            held_blocks = arrived
    attended_near = finish(pick_states(pair_states, 0))
    attended_far = finish(pick_states(pair_states, 1))
    for bit_index in range(seq_count.bit_length() - 1):
        attended_far = swapped(attended_far, "seq", bit_index)
    attended = jnp.concatenate([attended_near, attended_far], axis=0)
    weight_rows = lax.all_gather(proj_weight, "seq", axis=0, tiled=True)
    column_count = weight_rows.shape[1]
    blank_sum = jnp.zeros((exp_count, token_rows, split_count, column_count), jnp.float32)
    carried = blank_sum
    shard_piece = lax.all_gather(attended, "exp", axis=0, tiled=True)
    start_row = jnp.int32(0)
    shard_total = shard_piece.shape[0] // query_count
    for shard_index in range(shard_total):
        device_id = start_row // query_count + shard_index
        group_id = device_id % group_count
        half_id = device_id // group_count
        weight_slice = lax.dynamic_slice_in_dim(weight_rows, group_id * group_width, group_width, 0)
        rows_now = shard_piece[shard_index * query_count : (shard_index + 1) * query_count]
        product = jnp.dot(rows_now, weight_slice, preferred_element_type=jnp.float32)
        product = product.reshape(exp_count, token_rows, 1, column_count)
        corner = (0, 0, half_id, 0)
        present = lax.dynamic_slice(carried, corner, (exp_count, token_rows, 1, column_count))
        carried = lax.dynamic_update_slice(carried, present + product, corner)
    projected = carried
    projected = projected.reshape(block_len, column_count)
    attn_block = projected.astype(jnp.bfloat16)
    attn_update = lax.all_to_all(attn_block, "exp", split_axis=0, concat_axis=1, tiled=True)
    stream = residual.astype(jnp.float32) + attn_update.astype(jnp.float32)
    mean_sq = jnp.mean(stream * stream, axis=-1, keepdims=True)
    normed = (stream * lax.rsqrt(mean_sq + EPS) * norm_gain.astype(jnp.float32)).astype(
        jnp.bfloat16
    )
    logits = jnp.dot(normed, router, preferred_element_type=jnp.float32)
    expert_range = jnp.arange(EXPERTS, dtype=jnp.int32)
    picked = (expert_ids[:, :, None] == expert_range[None, None, :]).astype(jnp.float32)
    chosen = jnp.sum(picked * logits[:, None, :], axis=-1)
    mix_first = jax.nn.sigmoid(chosen[:, 0] - chosen[:, 1])
    mix_second = jax.nn.sigmoid(chosen[:, 1] - chosen[:, 0])
    piece_count = exp_count // EXPERTS
    piece_width = D // piece_count
    flat_ids = expert_ids.reshape(TOK_DEV * 2)
    member = (flat_ids[:, None] == expert_range[None, :]).astype(jnp.int32)
    slot_of = jnp.sum((jnp.cumsum(member, axis=0) - 1) * member, axis=1)
    token_of = jnp.arange(TOK_DEV * 2, dtype=jnp.int32) // 2
    slot_range = jnp.arange(CAP, dtype=jnp.int32)
    filled = member[:, :, None] * (slot_of[:, None, None] == slot_range[None, None, :]).astype(
        jnp.int32
    )
    source_token = jnp.sum(filled * token_of[:, None, None], axis=0)
    occupied = jnp.sum(filled, axis=0)
    piece_range = jnp.arange(piece_count, dtype=jnp.int32)
    take_index = source_token[:, None, :] * piece_count + piece_range[None, :, None]
    normed_rows = normed.reshape(TOK_DEV * piece_count, piece_width)
    send_rows = jnp.take(normed_rows, take_index, axis=0) * occupied[:, None, :, None].astype(
        jnp.bfloat16
    )
    send_rows = send_rows.reshape(exp_count, CAP, piece_width)
    dispatched = lax.all_to_all(send_rows, "exp", split_axis=0, concat_axis=0, tiled=True)
    expert_rows = dispatched.reshape(exp_count * CAP, piece_width)
    rank_sum = jnp.dot(expert_rows, u_gate_up[0], preferred_element_type=jnp.float32)
    for bit_index in range(piece_count.bit_length() - 1):
        rank_sum = rank_sum + swapped(rank_sum.astype(jnp.bfloat16), "exp", bit_index).astype(
            rank_sum.dtype
        )
    rank_in = rank_sum.astype(jnp.bfloat16)
    gate_part = jnp.dot(rank_in[:, :RANK], v_gate_up[0, 0], preferred_element_type=jnp.float32)
    up_part = jnp.dot(rank_in[:, RANK:], v_gate_up[0, 1], preferred_element_type=jnp.float32)
    hidden = (jax.nn.silu(gate_part) * up_part).astype(jnp.bfloat16)
    down_sum = jnp.dot(hidden, u_down[0], preferred_element_type=jnp.float32)
    for bit_index in range(piece_count.bit_length() - 1):
        down_sum = down_sum + swapped(down_sum.astype(jnp.bfloat16), "exp", bit_index).astype(
            down_sum.dtype
        )
    expert_out = jnp.dot(
        down_sum.astype(jnp.bfloat16), v_down[0], preferred_element_type=jnp.float32
    ).astype(jnp.bfloat16)
    returned = lax.all_to_all(
        expert_out.reshape(exp_count, CAP, piece_width),
        "exp",
        split_axis=0,
        concat_axis=0,
        tiled=True,
    )
    returned_rows = returned.reshape(exp_count * CAP, piece_width)
    slot_pairs = slot_of.reshape(TOK_DEV, 2)
    fetch_index = (
        expert_ids[:, :, None] * piece_count + piece_range[None, None, :]
    ) * CAP + slot_pairs[:, :, None]
    fetched = jnp.take(returned_rows, fetch_index, axis=0).astype(jnp.float32)
    fetched = fetched.reshape(TOK_DEV, 2, D)
    mixture = mix_first[:, None] * fetched[:, 0] + mix_second[:, None] * fetched[:, 1]
    return (stream + mixture).astype(jnp.bfloat16)


def solution(mesh):
    in_specs = (
        P(("seq", "exp"), None),
        P(("seq", "exp"), None),
        P(("seq", "exp"), None),
        P(("seq", "exp"), None),
        P("seq", "exp"),
        P(),
        P(),
        P(("seq", "exp"), None),
        P("exp", None, None),
        P("exp", None, None, None),
        P("exp", None, None),
        P("exp", None, None),
    )
    out_specs = P(("seq", "exp"), None)
    return jax.shard_map(
        per_device, mesh=mesh, in_specs=in_specs, out_specs=out_specs, check_vma=False
    )
```

profile of v0, /device:TPU:0, one launch (start us, length us, event | category | flops | bytes accessed | tf_op | source)
XLA Modules:
  0.0 555.5 jit_solution(10118629330337509046)
XLA Ops:
  8.2 6.4 %all-to-all-start.1 = ((bf16[128,8,128]{2,0,1:T(8,128)(2,1)}), bf16[128,8,128]{2,0,1:T(8,128)(2,1)S(1)}, u32[]{:S(2)}, u32[]{:S(2)}) async-start(bf16[128,8,128]{2,0,1:T(8,128)(2,1)} %bitcast.3), calls=%async_computation.1 | async-start | bytes 524288 | tf_op jit(solution)/shard_map/all_to_all | solution.py:132
  15.5 8.8 %all-to-all-done.1 = bf16[128,8,128]{2,0,1:T(8,128)(2,1)S(1)} async-done(((bf16[128,8,128]{2,0,1:T(8,128)(2,1)}), bf16[128,8,128]{2,0,1:T(8,128)(2,1)S(1)}, u32[]{:S(2)}, u32[]{:S(2)}) %all-to-all-start.1) | async-done | bytes 262176 | tf_op jit(solution)/shard_map/all_to_all | solution.py:132
  30.7 7.3 %all-to-all-done.2 = bf16[128,8,128]{2,0,1:T(8,128)(2,1)S(1)} async-done(((bf16[128,8,128]{2,0,1:T(8,128)(2,1)}), bf16[128,8,128]{2,0,1:T(8,128)(2,1)S(1)}, u32[]{:S(2)}, u32[]{:S(2)}) %all-to-all-start.2) | async-done | bytes 262176 | tf_op jit(solution)/shard_map/all_to_all | solution.py:133
  55.3 9.3 %collective-permute-done.5 = bf16[512,128]{1,0:T(8,128)(2,1)S(1)} collective-permute-done((bf16[512,128]{1,0:T(8,128)(2,1)S(1)}, bf16[512,128]{1,0:T(8,128)(2,1)S(1)}, u32[]{:S(2)}, u32[]{:S(2)}) %collective-permute-start.5) | collective-permute-done | bytes 131104 | tf_op jit(solution)/shard_map/ppermute | solution.py:19
  64.9 4.6 collective-permute-start.10
  73.5 4.3 collective-permute-done.9
  97.1 11.4 %collective-permute-done = bf16[512,3,128]{2,0,1:T(8,128)(2,1)} collective-permute-done((bf16[512,3,128]{2,0,1:T(8,128)(2,1)}, bf16[512,3,128]{2,0,1:T(8,128)(2,1)}, u32[]{:S(2)}, u32[]{:S(2)}) %collective-permute-start) | collective-permute-done | bytes 393248 | tf_op jit(solution)/shard_map/ppermute | solution.py:19
  113.3 15.1 %collective-permute-done.1 = bf16[512,3,128]{2,0,1:T(8,128)(2,1)S(1)} collective-permute-done((bf16[512,3,128]{2,0,1:T(8,128)(2,1)}, bf16[512,3,128]{2,0,1:T(8,128)(2,1)S(1)}, u32[]{:S(2)}, u32[]{:S(2)}) %collective-permute-start.1) | collective-permute-done | bytes 393248 | tf_op jit(solution)/shard_map/ppermute | solution.py:19
  147.0 7.8 %collective-permute-done.18 = bf16[512,384]{0,1:T(8,128)(2,1)S(1)} collective-permute-done((bf16[512,384]{0,1:T(8,128)(2,1)S(1)}, bf16[512,384]{0,1:T(8,128)(2,1)S(1)}, u32[]{:S(2)}, u32[]{:S(2)}) %collective-permute-start.18) | collective-permute-done | bytes 393248 | tf_op jit(solution)/shard_map/ppermute | solution.py:19
  155.7 7.4 %collective-permute-done.19 = bf16[512,384]{0,1:T(8,128)(2,1)S(1)} collective-permute-done((bf16[512,384]{0,1:T(8,128)(2,1)S(1)}, bf16[512,384]{0,1:T(8,128)(2,1)S(1)}, u32[]{:S(2)}, u32[]{:S(2)}) %collective-permute-start.19) | collective-permute-done | bytes 393248 | tf_op jit(solution)/shard_map/ppermute | solution.py:19
  164.1 63.2 %all-gather.3.cloned.1.call-done = bf16[8192,384]{0,1:T(8,128)(2,1)} async-done(((bf16[1024,384]{0,1:T(8,128)(2,1)}), bf16[8192,384]{0,1:T(8,128)(2,1)}) %all-gather.3.cloned.1.call-update) | async-done | bytes 6291472 | tf_op jit(solution)/shard_map/all_gather | solution.py:219
  249.4 34.8 %all-to-all-done.3 = bf16[8,128,768]{2,1,0:T(8,128)(2,1)S(1)} async-done(((bf16[8,128,768]{2,1,0:T(8,128)(2,1)}), bf16[8,128,768]{2,1,0:T(8,128)(2,1)S(1)}, u32[]{:S(2)}, u32[]{:S(2)}) %all-to-all-start.3) | async-done | bytes 1572896 | tf_op jit(solution)/shard_map/all_to_all | solution.py:236
  287.1 5.0 gather_fusion
  292.2 4.9 gather.13
  299.7 91.9 %all_to_all.68 = bf16[8,33,6144]{2,1,0:T(8,128)(2,1)} all-to-all(bf16[8,33,6144]{2,1,0:T(8,128)(2,1)S(1)} %select_multiply_fusion), channel_id=1, replica_groups=mesh['seq'=4,'exp'=8] {'exp'}, dimensions={0} | all-to-all | bytes 6488064 | tf_op jit(solution)/shard_map/all_to_all | solution.py:267
  391.5 5.0 reshape.493
  396.5 9.1 %fusion.80 = bf16[264,1024]{1,0:T(8,128)(2,1)S(1)} fusion(bf16[264,6144]{1,0:T(8,128)(2,1)} %reshape.493, bf16[1,6144,1024]{2,1,0:T(8,128)(2,1)} %param.20), kind=kOutput, calls=%fused_computation.117 | convolution fusion | flops 3322159104 | bytes 16367616 | tf_op jit(solution)/shard_map/dot_general | solution.py:269
  405.6 9.1 %fusion.6 = f32[264,8192]{1,0:T(8,128)} fusion(bf16[1,2,512,8192]{3,2,1,0:T(8,128)(2,1)} %param.21, bf16[264,1024]{1,0:T(8,128)(2,1)S(1)} %fusion.80), kind=kOutput, calls=%fused_computation.9 | convolution fusion | flops 2214592512 | bytes 17309696 | tf_op jit(solution)/shard_map/dot_general | solution.py:275
  414.8 11.2 %fusion.158 = bf16[264,512]{1,0:T(8,128)(2,1)S(1)} fusion(bf16[1,8192,512]{2,1,0:T(8,128)(2,1)} %param.22, f32[264,8192]{1,0:T(8,128)} %fusion.6, bf16[1,2,512,8192]{3,2,1,0:T(8,128)(2,1)} %param.21, bf16[264,1024]{1,0:T(8,128)(2,1)S(1)} %fusion.80), kind=kOutput, calls=%fused_computation.143 | convolution fusion | flops 4442296320 | bytes 25968640 | tf_op jit(solution)/shard_map/dot_general | solution.py:278
  425.9 6.4 %convolution_convert_fusion = bf16[264,6144]{1,0:T(8,128)(2,1)} fusion(bf16[264,512]{1,0:T(8,128)(2,1)S(1)} %fusion.158, bf16[1,512,6144]{2,1,0:T(8,128)(2,1)} %param.23), kind=kOutput, calls=%fused_computation.13 | convolution fusion | flops 1662566400 | bytes 9805824 | tf_op jit(solution)/shard_map/dot_general | solution.py:283
  432.3 4.9 reshape.494
  437.2 4.9 all-to-all-start.5
  443.2 87.3 %all-to-all-done.5 = bf16[8,33,6144]{2,1,0:T(8,128)(2,1)} async-done(((bf16[8,33,6144]{2,1,0:T(8,128)(2,1)}), bf16[8,33,6144]{2,1,0:T(8,128)(2,1)}, u32[]{:S(2)}, u32[]{:S(2)}) %all-to-all-start.5) | async-done | bytes 3244064 | tf_op jit(solution)/shard_map/all_to_all | solution.py:286
  537.8 5.9 %gather.15 = bf16[128,2,6144]{2,1,0:T(2,128)(2,1)S(1)} reshape(bf16[256,6144]{1,0:T(8,128)(2,1)} %gather_fusion.1) | data formatting | bytes 6291456 | tf_op jit(solution)/shard_map/jit(_take)/gather | solution.py:298
  (205 shorter events, 114.9 us)
Async XLA Ops:
  8.2 16.1 %all-to-all-start.1 = ((bf16[128,8,128]{2,0,1:T(8,128)(2,1)}), bf16[128,8,128]{2,0,1:T(8,128)(2,1)S(1)}, u32[]{:S(2)}, u32[]{:S(2)}) async-start(bf16[128,8,128]{2,0,1:T(8,128)(2,1)} %bitcast.3), calls=%async_computation.1 | async-start | bytes 524288 | tf_op jit(solution)/shard_map/all_to_all | solution.py:132
  25.0 13.1 %all-to-all-start.2 = ((bf16[128,8,128]{2,0,1:T(8,128)(2,1)}), bf16[128,8,128]{2,0,1:T(8,128)(2,1)S(1)}, u32[]{:S(2)}, u32[]{:S(2)}) async-start(bf16[128,8,128]{2,0,1:T(8,128)(2,1)} %bitcast.8), calls=%async_computation.2 | async-start | bytes 524288 | tf_op jit(solution)/shard_map/all_to_all | solution.py:133
  38.0 53.9 %all-to-all-start = ((bf16[128,8,384]{0,2,1:T(8,128)(2,1)}), bf16[128,8,384]{0,2,1:T(8,128)(2,1)S(1)}, u32[]{:S(2)}, u32[]{:S(2)}) async-start(bf16[128,8,384]{0,2,1:T(8,128)(2,1)} %bitcast), calls=%async_computation | async-start | bytes 1572864 | tf_op jit(solution)/shard_map/all_to_all | solution.py:131
  41.6 122.5 %all-gather.5.cloned.1.call-start = ((), (), s32[]{:S(2)}) async-start(), calls=%async_computation.7 | async-start | bytes 5898240 | tf_op jit(solution)/shard_map/all_gather | solution.py:215
  43.9 183.4 %all-gather.3.cloned.1.call-start = ((), (), s32[]{:S(2)}) async-start(), calls=%async_computation.6 | async-start | bytes 7077888 | tf_op jit(solution)/shard_map/all_gather | solution.py:219
  50.3 14.3 %collective-permute-start.5 = (bf16[512,128]{1,0:T(8,128)(2,1)S(1)}, bf16[512,128]{1,0:T(8,128)(2,1)S(1)}, u32[]{:S(2)}, u32[]{:S(2)}) collective-permute-start(bf16[512,128]{1,0:T(8,128)(2,1)S(1)} %collective-permute-done.4), channel_id=1, source_target_pairs={{0,16},{8,24},{16,0},{24,8},{1,17},{9,25},{17,1},{25,9},{2,18},{10... | collective-permute-start | bytes 393224 | tf_op jit(solution)/shard_map/ppermute | solution.py:19
  51.8 13.0 %collective-permute-start.6 = (bf16[512,128]{1,0:T(8,128)(2,1)S(1)}, bf16[512,128]{1,0:T(8,128)(2,1)S(1)}, u32[]{:S(2)}, u32[]{:S(2)}) collective-permute-start(bf16[512,128]{1,0:T(8,128)(2,1)S(1)} %bitcast.398), channel_id=1, source_target_pairs={{0,8},{8,16},{16,24},{24,0},{1,9},{9,17},{17,25},{25,1},{2,10},{10... | collective-permute-start | bytes 393224 | tf_op jit(solution)/shard_map/ppermute | solution.py:25
  53.3 16.1 %collective-permute-start.8 = (bf16[512,128]{1,0:T(8,128)(2,1)S(1)}, bf16[512,128]{1,0:T(8,128)(2,1)S(1)}, u32[]{:S(2)}, u32[]{:S(2)}) collective-permute-start(bf16[512,128]{1,0:T(8,128)(2,1)S(1)} %bitcast.403), channel_id=1, source_target_pairs={{0,8},{8,16},{16,24},{24,0},{1,9},{9,17},{17,25},{25,1},{2,10},{10... | collective-permute-start | bytes 393224 | tf_op jit(solution)/shard_map/ppermute | solution.py:25
  53.8 18.4 %collective-permute-start.7 = (bf16[512,128]{1,0:T(8,128)(2,1)S(1)}, bf16[512,128]{1,0:T(8,128)(2,1)S(1)}, u32[]{:S(2)}, u32[]{:S(2)}) collective-permute-start(bf16[512,128]{1,0:T(8,128)(2,1)S(1)} %collective-permute-done.3), channel_id=1, source_target_pairs={{0,8},{8,16},{16,24},{24,0},{1,9},{9,17},{17,25},{25,1},{2,10},{10... | collective-permute-start | bytes 393224 | tf_op jit(solution)/shard_map/ppermute | solution.py:25
  64.6 13.2 %collective-permute-start.9 = (bf16[512,128]{1,0:T(8,128)(2,1)S(1)}, bf16[512,128]{1,0:T(8,128)(2,1)S(1)}, u32[]{:S(2)}, u32[]{:S(2)}) collective-permute-start(bf16[512,128]{1,0:T(8,128)(2,1)S(1)} %collective-permute-done.5), channel_id=1, source_target_pairs={{0,8},{8,16},{16,24},{24,0},{1,9},{9,17},{17,25},{25,1},{2,10},{10... | collective-permute-start | bytes 393224 | tf_op jit(solution)/shard_map/ppermute | solution.py:25
  64.9 18.1 %collective-permute-start.10 = (bf16[512,128]{1,0:T(8,128)(2,1)S(1)}, bf16[512,128]{1,0:T(8,128)(2,1)S(1)}, u32[]{:S(2)}, u32[]{:S(2)}) collective-permute-start(bf16[512,128]{1,0:T(8,128)(2,1)S(1)} %collective-permute-done.6), channel_id=1, source_target_pairs={{0,8},{8,16},{16,24},{24,0},{1,9},{9,17},{17,25},{25,1},{2,10},{10... | collective-permute-start | bytes 393224 | tf_op jit(solution)/shard_map/ppermute | solution.py:25
  69.4 16.4 %collective-permute-start.12 = (bf16[512,128]{1,0:T(8,128)(2,1)S(1)}, bf16[512,128]{1,0:T(8,128)(2,1)S(1)}, u32[]{:S(2)}, u32[]{:S(2)}) collective-permute-start(bf16[512,128]{1,0:T(8,128)(2,1)S(1)} %collective-permute-done.8), channel_id=1, source_target_pairs={{0,8},{8,16},{16,24},{24,0},{1,9},{9,17},{17,25},{25,1},{2,10},{10... | collective-permute-start | bytes 393224 | tf_op jit(solution)/shard_map/ppermute | solution.py:25
  72.2 16.4 %collective-permute-start.11 = (bf16[512,128]{1,0:T(8,128)(2,1)S(1)}, bf16[512,128]{1,0:T(8,128)(2,1)S(1)}, u32[]{:S(2)}, u32[]{:S(2)}) collective-permute-start(bf16[512,128]{1,0:T(8,128)(2,1)S(1)} %collective-permute-done.7), channel_id=1, source_target_pairs={{0,8},{8,16},{16,24},{24,0},{1,9},{9,17},{17,25},{25,1},{2,10},{10... | collective-permute-start | bytes 393224 | tf_op jit(solution)/shard_map/ppermute | solution.py:25
  77.8 13.6 %collective-permute-start.13 = (bf16[512,128]{1,0:T(8,128)(2,1)S(1)}, bf16[512,128]{1,0:T(8,128)(2,1)S(1)}, u32[]{:S(2)}, u32[]{:S(2)}) collective-permute-start(bf16[512,128]{1,0:T(8,128)(2,1)S(1)} %collective-permute-done.9), channel_id=1, source_target_pairs={{0,8},{8,16},{16,24},{24,0},{1,9},{9,17},{17,25},{25,1},{2,10},{10... | collective-permute-start | bytes 393224 | tf_op jit(solution)/shard_map/ppermute | solution.py:25
  83.0 57.6 %collective-permute-start.14 = (bf16[512,128]{1,0:T(8,128)(2,1)S(1)}, bf16[512,128]{1,0:T(8,128)(2,1)S(1)}, u32[]{:S(2)}, u32[]{:S(2)}) collective-permute-start(bf16[512,128]{1,0:T(8,128)(2,1)S(1)} %collective-permute-done.10), channel_id=1, source_target_pairs={{0,8},{8,16},{16,24},{24,0},{1,9},{9,17},{17,25},{25,1},{2,10},{10... | collective-permute-start | bytes 393224 | tf_op jit(solution)/shard_map/ppermute | solution.py:25
  85.8 56.3 %collective-permute-start.16 = (bf16[512,128]{1,0:T(8,128)(2,1)S(1)}, bf16[512,128]{1,0:T(8,128)(2,1)S(1)}, u32[]{:S(2)}, u32[]{:S(2)}) collective-permute-start(bf16[512,128]{1,0:T(8,128)(2,1)S(1)} %collective-permute-done.12), channel_id=1, source_target_pairs={{0,8},{8,16},{16,24},{24,0},{1,9},{9,17},{17,25},{25,1},{2,10},{10... | collective-permute-start | bytes 393224 | tf_op jit(solution)/shard_map/ppermute | solution.py:25
  88.6 52.0 %collective-permute-start.15 = (bf16[512,128]{1,0:T(8,128)(2,1)S(1)}, bf16[512,128]{1,0:T(8,128)(2,1)S(1)}, u32[]{:S(2)}, u32[]{:S(2)}) collective-permute-start(bf16[512,128]{1,0:T(8,128)(2,1)S(1)} %collective-permute-done.11), channel_id=1, source_target_pairs={{0,8},{8,16},{16,24},{24,0},{1,9},{9,17},{17,25},{25,1},{2,10},{10... | collective-permute-start | bytes 393224 | tf_op jit(solution)/shard_map/ppermute | solution.py:25
  91.4 50.7 %collective-permute-start.17 = (bf16[512,128]{1,0:T(8,128)(2,1)S(1)}, bf16[512,128]{1,0:T(8,128)(2,1)S(1)}, u32[]{:S(2)}, u32[]{:S(2)}) collective-permute-start(bf16[512,128]{1,0:T(8,128)(2,1)S(1)} %collective-permute-done.13), channel_id=1, source_target_pairs={{0,8},{8,16},{16,24},{24,0},{1,9},{9,17},{17,25},{25,1},{2,10},{10... | collective-permute-start | bytes 393224 | tf_op jit(solution)/shard_map/ppermute | solution.py:25
  93.4 15.2 %collective-permute-start = (bf16[512,3,128]{2,0,1:T(8,128)(2,1)}, bf16[512,3,128]{2,0,1:T(8,128)(2,1)}, u32[]{:S(2)}, u32[]{:S(2)}) collective-permute-start(bf16[512,3,128]{2,0,1:T(8,128)(2,1)} %copy.188), channel_id=1, source_target_pairs={{0,8},{8,0},{16,24},{24,16},{1,9},{9,1},{17,25},{25,17},{2,10},{10... | collective-permute-start | bytes 1179656 | tf_op jit(solution)/shard_map/ppermute | solution.py:19
  108.5 19.9 %collective-permute-start.1 = (bf16[512,3,128]{2,0,1:T(8,128)(2,1)}, bf16[512,3,128]{2,0,1:T(8,128)(2,1)S(1)}, u32[]{:S(2)}, u32[]{:S(2)}) collective-permute-start(bf16[512,3,128]{2,0,1:T(8,128)(2,1)} %collective-permute-done), channel_id=1, source_target_pairs={{0,16},{8,24},{16,0},{24,8},{1,17},{9,25},{17,1},{25,9},{2,18},{10... | collective-permute-start | bytes 1179656 | tf_op jit(solution)/shard_map/ppermute | solution.py:19
  145.7 9.1 %collective-permute-start.18 = (bf16[512,384]{0,1:T(8,128)(2,1)S(1)}, bf16[512,384]{0,1:T(8,128)(2,1)S(1)}, u32[]{:S(2)}, u32[]{:S(2)}) collective-permute-start(bf16[512,384]{0,1:T(8,128)(2,1)S(1)} %fusion.181), channel_id=1, source_target_pairs={{0,8},{8,0},{16,24},{24,16},{1,9},{9,1},{17,25},{25,17},{2,10},{10... | collective-permute-start | bytes 1179656 | tf_op jit(solution)/shard_map/ppermute | solution.py:19
  154.8 8.2 %collective-permute-start.19 = (bf16[512,384]{0,1:T(8,128)(2,1)S(1)}, bf16[512,384]{0,1:T(8,128)(2,1)S(1)}, u32[]{:S(2)}, u32[]{:S(2)}) collective-permute-start(bf16[512,384]{0,1:T(8,128)(2,1)S(1)} %collective-permute-done.18), channel_id=1, source_target_pairs={{0,16},{8,24},{16,0},{24,8},{1,17},{9,25},{17,1},{25,9},{2,18},{10... | collective-permute-start | bytes 1179656 | tf_op jit(solution)/shard_map/ppermute | solution.py:19
  242.7 41.4 %all-to-all-start.3 = ((bf16[8,128,768]{2,1,0:T(8,128)(2,1)}), bf16[8,128,768]{2,1,0:T(8,128)(2,1)S(1)}, u32[]{:S(2)}, u32[]{:S(2)}) async-start(bf16[8,128,768]{2,1,0:T(8,128)(2,1)} %bitcast.89), calls=%async_computation.3 | async-start | bytes 3145728 | tf_op jit(solution)/shard_map/all_to_all | solution.py:236
  437.2 93.2 %all-to-all-start.5 = ((bf16[8,33,6144]{2,1,0:T(8,128)(2,1)}), bf16[8,33,6144]{2,1,0:T(8,128)(2,1)}, u32[]{:S(2)}, u32[]{:S(2)}) async-start(bf16[8,33,6144]{2,1,0:T(8,128)(2,1)} %reshape.494), calls=%async_computation.5 | async-start | bytes 7864320 | tf_op jit(solution)/shard_map/all_to_all | solution.py:286
  (20 other events, 117.3 us)
Sparse Core Ops, SparseCore 0:
  44.3 99.9 all-gather.4
  164.2 63.0 all-gather.2
where the time goes:
time: 560 us; the launch traced here: 556 us
  waiting for transfers between devices  275 us (49%)
  blocking collectives  91.9 us (16%)
  matrix products  66.4 us (12%)
  local copies, waits for them, and re-layouts  45.2 us (8%)
  starting transfers between devices  44 us (8%)
  other arithmetic  18.2 us (3%)
  between operations  14.6 us (3%)
    all_to_all x1, blocking collectives, per_device(): lax.all_to_all(send_rows, 'exp', split_axis=0, concat_axis=0, tiled=True)  91.9 us
    all_to_all x1, waiting for transfers between devices, per_device(): lax.all_to_all(expert_out.reshape(exp_count, CAP, piece_width), 'exp', sp...  87.3 us
    all_gather x1, waiting for transfers between devices, per_device(): shard_piece = lax.all_gather(attended, 'exp', axis=0, tiled=True)  63.2 us
    ppermute x8, waiting for transfers between devices, swapped(): lax.ppermute(x, axis, [(i, i ^ 1 << distance) for i in range(lax.axis_siz...  55.8 us
    all_to_all x1, waiting for transfers between devices, per_device(): lax.all_to_all(attn_block, 'exp', split_axis=0, concat_axis=1, tiled=True)  34.8 us
    ppermute x12, waiting for transfers between devices, passed_along(): return lax.ppermute(value, axis, pairs)  18.1 us
    dot_general x8, matrix products, per_device(): jnp.dot(rows_now, weight_slice, preferred_element_type=jnp.float32)  15.3 us
    ppermute x12, starting transfers between devices, passed_along(): return lax.ppermute(value, axis, pairs)  12.2 us
  transfers between devices with their start and end apart: 27, of which 18 were waited for; matrix products, arithmetic and copies ran while one was open for 6% of the time, Pallas kernels for 0%

commit v1 on v0

--- a/solution.py
+++ b/solution.py
@@ -233,7 +233,9 @@
     projected = carried
     projected = projected.reshape(block_len, column_count)
     attn_block = projected.astype(jnp.bfloat16)
-    attn_update = lax.all_to_all(attn_block, "exp", split_axis=0, concat_axis=1, tiled=True)
+    parts = jnp.split(attn_block, lax.axis_size("exp"), axis=0)
+    received = lax.all_to_all(jnp.stack(parts), "exp", 0, 0)
+    attn_update = jnp.concatenate(received, axis=1)
     stream = residual.astype(jnp.float32) + attn_update.astype(jnp.float32)
     mean_sq = jnp.mean(stream * stream, axis=-1, keepdims=True)
     normed = (stream * lax.rsqrt(mean_sq + EPS) * norm_gain.astype(jnp.float32)).astype(

time: 560 us -> 574 us (1.025)
  local copies, waits for them, and re-layouts: 45.2 us -> 53.8 us
  other arithmetic: 18.2 us -> 24 us
where the time goes in v1:
time: 574 us; the launch traced here: 570 us
  waiting for transfers between devices  275 us (48%)
  blocking collectives  91.9 us (16%)
  matrix products  65.4 us (11%)
  local copies, waits for them, and re-layouts  53.8 us (9%)
  starting transfers between devices  44.6 us (8%)
  other arithmetic  24 us (4%)
  between operations  14.6 us (3%)
    all_to_all x1, blocking collectives, per_device(): lax.all_to_all(send_rows, 'exp', split_axis=0, concat_axis=0, tiled=True)  91.9 us
    all_to_all x1, waiting for transfers between devices, per_device(): lax.all_to_all(expert_out.reshape(exp_count, CAP, piece_width), 'exp', sp...  87.3 us
    all_gather x1, waiting for transfers between devices, per_device(): shard_piece = lax.all_gather(attended, 'exp', axis=0, tiled=True)  63.2 us
    ppermute x8, waiting for transfers between devices, swapped(): lax.ppermute(x, axis, [(i, i ^ 1 << distance) for i in range(lax.axis_siz...  55.8 us
    all_to_all x1, waiting for transfers between devices, per_device(): received = lax.all_to_all(jnp.stack(parts), 'exp', 0, 0)  34.8 us
    ppermute x12, waiting for transfers between devices, passed_along(): return lax.ppermute(value, axis, pairs)  18.1 us
    dot_general x8, matrix products, per_device(): jnp.dot(rows_now, weight_slice, preferred_element_type=jnp.float32)  14.4 us
    ppermute x12, starting transfers between devices, passed_along(): return lax.ppermute(value, axis, pairs)  12.2 us
  transfers between devices with their start and end apart: 27, of which 18 were waited for; matrix products, arithmetic and copies ran while one was open for 6% of the time, Pallas kernels for 0%

profile of v1, /device:TPU:0, one launch (start us, length us, event | category | flops | bytes accessed | tf_op | source)
XLA Modules:
  0.0 569.7 jit_solution(16537191967519510445)
XLA Ops:
  8.2 6.4 %all-to-all-start.1 = ((bf16[128,8,128]{2,0,1:T(8,128)(2,1)}), bf16[128,8,128]{2,0,1:T(8,128)(2,1)S(1)}, u32[]{:S(2)}, u32[]{:S(2)}) async-start(bf16[128,8,128]{2,0,1:T(8,128)(2,1)} %bitcast.3), calls=%async_computation.1 | async-start | bytes 524288 | tf_op jit(solution)/shard_map/all_to_all | solution.py:132
  15.5 8.8 %all-to-all-done.1 = bf16[128,8,128]{2,0,1:T(8,128)(2,1)S(1)} async-done(((bf16[128,8,128]{2,0,1:T(8,128)(2,1)}), bf16[128,8,128]{2,0,1:T(8,128)(2,1)S(1)}, u32[]{:S(2)}, u32[]{:S(2)}) %all-to-all-start.1) | async-done | bytes 262176 | tf_op jit(solution)/shard_map/all_to_all | solution.py:132
  30.7 7.3 %all-to-all-done.2 = bf16[128,8,128]{2,0,1:T(8,128)(2,1)S(1)} async-done(((bf16[128,8,128]{2,0,1:T(8,128)(2,1)}), bf16[128,8,128]{2,0,1:T(8,128)(2,1)S(1)}, u32[]{:S(2)}, u32[]{:S(2)}) %all-to-all-start.2) | async-done | bytes 262176 | tf_op jit(solution)/shard_map/all_to_all | solution.py:133
  55.3 9.3 %collective-permute-done.5 = bf16[512,128]{1,0:T(8,128)(2,1)S(1)} collective-permute-done((bf16[512,128]{1,0:T(8,128)(2,1)S(1)}, bf16[512,128]{1,0:T(8,128)(2,1)S(1)}, u32[]{:S(2)}, u32[]{:S(2)}) %collective-permute-start.5) | collective-permute-done | bytes 131104 | tf_op jit(solution)/shard_map/ppermute | solution.py:19
  64.9 4.6 collective-permute-start.10
  73.5 4.3 collective-permute-done.9
  97.1 11.4 %collective-permute-done = bf16[512,3,128]{2,0,1:T(8,128)(2,1)} collective-permute-done((bf16[512,3,128]{2,0,1:T(8,128)(2,1)}, bf16[512,3,128]{2,0,1:T(8,128)(2,1)}, u32[]{:S(2)}, u32[]{:S(2)}) %collective-permute-start) | collective-permute-done | bytes 393248 | tf_op jit(solution)/shard_map/ppermute | solution.py:19
  113.3 15.1 %collective-permute-done.1 = bf16[512,3,128]{2,0,1:T(8,128)(2,1)S(1)} collective-permute-done((bf16[512,3,128]{2,0,1:T(8,128)(2,1)}, bf16[512,3,128]{2,0,1:T(8,128)(2,1)S(1)}, u32[]{:S(2)}, u32[]{:S(2)}) %collective-permute-start.1) | collective-permute-done | bytes 393248 | tf_op jit(solution)/shard_map/ppermute | solution.py:19
  147.0 7.8 %collective-permute-done.18 = bf16[512,384]{0,1:T(8,128)(2,1)S(1)} collective-permute-done((bf16[512,384]{0,1:T(8,128)(2,1)S(1)}, bf16[512,384]{0,1:T(8,128)(2,1)S(1)}, u32[]{:S(2)}, u32[]{:S(2)}) %collective-permute-start.18) | collective-permute-done | bytes 393248 | tf_op jit(solution)/shard_map/ppermute | solution.py:19
  155.7 7.4 %collective-permute-done.19 = bf16[512,384]{0,1:T(8,128)(2,1)S(1)} collective-permute-done((bf16[512,384]{0,1:T(8,128)(2,1)S(1)}, bf16[512,384]{0,1:T(8,128)(2,1)S(1)}, u32[]{:S(2)}, u32[]{:S(2)}) %collective-permute-start.19) | collective-permute-done | bytes 393248 | tf_op jit(solution)/shard_map/ppermute | solution.py:19
  164.1 63.2 %all-gather.3.cloned.1.call-done = bf16[8192,384]{0,1:T(8,128)(2,1)} async-done(((bf16[1024,384]{0,1:T(8,128)(2,1)}), bf16[8192,384]{0,1:T(8,128)(2,1)}) %all-gather.3.cloned.1.call-update) | async-done | bytes 6291472 | tf_op jit(solution)/shard_map/all_gather | solution.py:219
  254.5 34.8 %all-to-all-done.3 = bf16[8,128,768]{2,1,0:T(8,128)(2,1)} async-done(((bf16[8,128,768]{2,1,0:T(8,128)(2,1)}), bf16[8,128,768]{2,1,0:T(8,128)(2,1)}, u32[]{:S(2)}, u32[]{:S(2)}) %all-to-all-start.3) | async-done | bytes 1572896 | tf_op jit(solution)/shard_map/all_to_all | solution.py:237
  301.3 5.0 gather_fusion
  306.3 4.9 gather.13
  313.8 91.9 %all_to_all.60 = bf16[8,33,6144]{2,1,0:T(8,128)(2,1)} all-to-all(bf16[8,33,6144]{2,1,0:T(8,128)(2,1)S(1)} %select_multiply_fusion), channel_id=1, replica_groups=mesh['seq'=4,'exp'=8] {'exp'}, dimensions={0} | all-to-all | bytes 6488064 | tf_op jit(solution)/shard_map/all_to_all | solution.py:269
  405.7 5.0 reshape.492
  410.7 9.1 %fusion.80 = bf16[264,1024]{1,0:T(8,128)(2,1)S(1)} fusion(bf16[264,6144]{1,0:T(8,128)(2,1)} %reshape.492, bf16[1,6144,1024]{2,1,0:T(8,128)(2,1)} %param.20), kind=kOutput, calls=%fused_computation.117 | convolution fusion | flops 3322159104 | bytes 16367616 | tf_op jit(solution)/shard_map/dot_general | solution.py:271
  419.8 9.1 %fusion.6 = f32[264,8192]{1,0:T(8,128)} fusion(bf16[1,2,512,8192]{3,2,1,0:T(8,128)(2,1)} %param.21, bf16[264,1024]{1,0:T(8,128)(2,1)S(1)} %fusion.80), kind=kOutput, calls=%fused_computation.9 | convolution fusion | flops 2214592512 | bytes 17309696 | tf_op jit(solution)/shard_map/dot_general | solution.py:277
  428.9 11.2 %fusion.158 = bf16[264,512]{1,0:T(8,128)(2,1)S(1)} fusion(bf16[1,8192,512]{2,1,0:T(8,128)(2,1)} %param.22, f32[264,8192]{1,0:T(8,128)} %fusion.6, bf16[1,2,512,8192]{3,2,1,0:T(8,128)(2,1)} %param.21, bf16[264,1024]{1,0:T(8,128)(2,1)S(1)} %fusion.80), kind=kOutput, calls=%fused_computation.143 | convolution fusion | flops 4442296320 | bytes 25968640 | tf_op jit(solution)/shard_map/dot_general | solution.py:280
  440.1 6.4 %convolution_convert_fusion = bf16[264,6144]{1,0:T(8,128)(2,1)} fusion(bf16[264,512]{1,0:T(8,128)(2,1)S(1)} %fusion.158, bf16[1,512,6144]{2,1,0:T(8,128)(2,1)} %param.23), kind=kOutput, calls=%fused_computation.13 | convolution fusion | flops 1662566400 | bytes 9805824 | tf_op jit(solution)/shard_map/dot_general | solution.py:285
  446.4 4.9 reshape.493
  451.4 4.9 all-to-all-start.5
  457.3 87.3 %all-to-all-done.5 = bf16[8,33,6144]{2,1,0:T(8,128)(2,1)} async-done(((bf16[8,33,6144]{2,1,0:T(8,128)(2,1)}), bf16[8,33,6144]{2,1,0:T(8,128)(2,1)}, u32[]{:S(2)}, u32[]{:S(2)}) %all-to-all-start.5) | async-done | bytes 3244064 | tf_op jit(solution)/shard_map/all_to_all | solution.py:288
  552.0 5.9 %gather.15 = bf16[128,2,6144]{2,1,0:T(2,128)(2,1)S(1)} reshape(bf16[256,6144]{1,0:T(8,128)(2,1)} %gather_fusion.1) | data formatting | bytes 6291456 | tf_op jit(solution)/shard_map/jit(_take)/gather | solution.py:300
  (214 shorter events, 129.0 us)
Async XLA Ops:
  8.2 16.1 %all-to-all-start.1 = ((bf16[128,8,128]{2,0,1:T(8,128)(2,1)}), bf16[128,8,128]{2,0,1:T(8,128)(2,1)S(1)}, u32[]{:S(2)}, u32[]{:S(2)}) async-start(bf16[128,8,128]{2,0,1:T(8,128)(2,1)} %bitcast.3), calls=%async_computation.1 | async-start | bytes 524288 | tf_op jit(solution)/shard_map/all_to_all | solution.py:132
  25.0 13.1 %all-to-all-start.2 = ((bf16[128,8,128]{2,0,1:T(8,128)(2,1)}), bf16[128,8,128]{2,0,1:T(8,128)(2,1)S(1)}, u32[]{:S(2)}, u32[]{:S(2)}) async-start(bf16[128,8,128]{2,0,1:T(8,128)(2,1)} %bitcast.8), calls=%async_computation.2 | async-start | bytes 524288 | tf_op jit(solution)/shard_map/all_to_all | solution.py:133
  38.0 53.9 %all-to-all-start = ((bf16[128,8,384]{0,2,1:T(8,128)(2,1)}), bf16[128,8,384]{0,2,1:T(8,128)(2,1)S(1)}, u32[]{:S(2)}, u32[]{:S(2)}) async-start(bf16[128,8,384]{0,2,1:T(8,128)(2,1)} %bitcast), calls=%async_computation | async-start | bytes 1572864 | tf_op jit(solution)/shard_map/all_to_all | solution.py:131
  41.6 122.5 %all-gather.5.cloned.1.call-start = ((), (), s32[]{:S(2)}) async-start(), calls=%async_computation.7 | async-start | bytes 5898240 | tf_op jit(solution)/shard_map/all_gather | solution.py:215
  43.9 183.4 %all-gather.3.cloned.1.call-start = ((), (), s32[]{:S(2)}) async-start(), calls=%async_computation.6 | async-start | bytes 7077888 | tf_op jit(solution)/shard_map/all_gather | solution.py:219
  50.3 14.3 %collective-permute-start.5 = (bf16[512,128]{1,0:T(8,128)(2,1)S(1)}, bf16[512,128]{1,0:T(8,128)(2,1)S(1)}, u32[]{:S(2)}, u32[]{:S(2)}) collective-permute-start(bf16[512,128]{1,0:T(8,128)(2,1)S(1)} %collective-permute-done.4), channel_id=1, source_target_pairs={{0,16},{8,24},{16,0},{24,8},{1,17},{9,25},{17,1},{25,9},{2,18},{10... | collective-permute-start | bytes 393224 | tf_op jit(solution)/shard_map/ppermute | solution.py:19
  51.8 13.0 %collective-permute-start.6 = (bf16[512,128]{1,0:T(8,128)(2,1)S(1)}, bf16[512,128]{1,0:T(8,128)(2,1)S(1)}, u32[]{:S(2)}, u32[]{:S(2)}) collective-permute-start(bf16[512,128]{1,0:T(8,128)(2,1)S(1)} %bitcast.426), channel_id=1, source_target_pairs={{0,8},{8,16},{16,24},{24,0},{1,9},{9,17},{17,25},{25,1},{2,10},{10... | collective-permute-start | bytes 393224 | tf_op jit(solution)/shard_map/ppermute | solution.py:25
  53.3 16.1 %collective-permute-start.8 = (bf16[512,128]{1,0:T(8,128)(2,1)S(1)}, bf16[512,128]{1,0:T(8,128)(2,1)S(1)}, u32[]{:S(2)}, u32[]{:S(2)}) collective-permute-start(bf16[512,128]{1,0:T(8,128)(2,1)S(1)} %bitcast.431), channel_id=1, source_target_pairs={{0,8},{8,16},{16,24},{24,0},{1,9},{9,17},{17,25},{25,1},{2,10},{10... | collective-permute-start | bytes 393224 | tf_op jit(solution)/shard_map/ppermute | solution.py:25
  53.8 18.4 %collective-permute-start.7 = (bf16[512,128]{1,0:T(8,128)(2,1)S(1)}, bf16[512,128]{1,0:T(8,128)(2,1)S(1)}, u32[]{:S(2)}, u32[]{:S(2)}) collective-permute-start(bf16[512,128]{1,0:T(8,128)(2,1)S(1)} %collective-permute-done.3), channel_id=1, source_target_pairs={{0,8},{8,16},{16,24},{24,0},{1,9},{9,17},{17,25},{25,1},{2,10},{10... | collective-permute-start | bytes 393224 | tf_op jit(solution)/shard_map/ppermute | solution.py:25
  64.6 13.2 %collective-permute-start.9 = (bf16[512,128]{1,0:T(8,128)(2,1)S(1)}, bf16[512,128]{1,0:T(8,128)(2,1)S(1)}, u32[]{:S(2)}, u32[]{:S(2)}) collective-permute-start(bf16[512,128]{1,0:T(8,128)(2,1)S(1)} %collective-permute-done.5), channel_id=1, source_target_pairs={{0,8},{8,16},{16,24},{24,0},{1,9},{9,17},{17,25},{25,1},{2,10},{10... | collective-permute-start | bytes 393224 | tf_op jit(solution)/shard_map/ppermute | solution.py:25
  64.9 18.1 %collective-permute-start.10 = (bf16[512,128]{1,0:T(8,128)(2,1)S(1)}, bf16[512,128]{1,0:T(8,128)(2,1)S(1)}, u32[]{:S(2)}, u32[]{:S(2)}) collective-permute-start(bf16[512,128]{1,0:T(8,128)(2,1)S(1)} %collective-permute-done.6), channel_id=1, source_target_pairs={{0,8},{8,16},{16,24},{24,0},{1,9},{9,17},{17,25},{25,1},{2,10},{10... | collective-permute-start | bytes 393224 | tf_op jit(solution)/shard_map/ppermute | solution.py:25
  69.4 16.4 %collective-permute-start.12 = (bf16[512,128]{1,0:T(8,128)(2,1)S(1)}, bf16[512,128]{1,0:T(8,128)(2,1)S(1)}, u32[]{:S(2)}, u32[]{:S(2)}) collective-permute-start(bf16[512,128]{1,0:T(8,128)(2,1)S(1)} %collective-permute-done.8), channel_id=1, source_target_pairs={{0,8},{8,16},{16,24},{24,0},{1,9},{9,17},{17,25},{25,1},{2,10},{10... | collective-permute-start | bytes 393224 | tf_op jit(solution)/shard_map/ppermute | solution.py:25
  72.2 16.4 %collective-permute-start.11 = (bf16[512,128]{1,0:T(8,128)(2,1)S(1)}, bf16[512,128]{1,0:T(8,128)(2,1)S(1)}, u32[]{:S(2)}, u32[]{:S(2)}) collective-permute-start(bf16[512,128]{1,0:T(8,128)(2,1)S(1)} %collective-permute-done.7), channel_id=1, source_target_pairs={{0,8},{8,16},{16,24},{24,0},{1,9},{9,17},{17,25},{25,1},{2,10},{10... | collective-permute-start | bytes 393224 | tf_op jit(solution)/shard_map/ppermute | solution.py:25
  77.8 13.6 %collective-permute-start.13 = (bf16[512,128]{1,0:T(8,128)(2,1)S(1)}, bf16[512,128]{1,0:T(8,128)(2,1)S(1)}, u32[]{:S(2)}, u32[]{:S(2)}) collective-permute-start(bf16[512,128]{1,0:T(8,128)(2,1)S(1)} %collective-permute-done.9), channel_id=1, source_target_pairs={{0,8},{8,16},{16,24},{24,0},{1,9},{9,17},{17,25},{25,1},{2,10},{10... | collective-permute-start | bytes 393224 | tf_op jit(solution)/shard_map/ppermute | solution.py:25
  83.0 57.6 %collective-permute-start.14 = (bf16[512,128]{1,0:T(8,128)(2,1)S(1)}, bf16[512,128]{1,0:T(8,128)(2,1)S(1)}, u32[]{:S(2)}, u32[]{:S(2)}) collective-permute-start(bf16[512,128]{1,0:T(8,128)(2,1)S(1)} %collective-permute-done.10), channel_id=1, source_target_pairs={{0,8},{8,16},{16,24},{24,0},{1,9},{9,17},{17,25},{25,1},{2,10},{10... | collective-permute-start | bytes 393224 | tf_op jit(solution)/shard_map/ppermute | solution.py:25
  85.8 56.3 %collective-permute-start.16 = (bf16[512,128]{1,0:T(8,128)(2,1)S(1)}, bf16[512,128]{1,0:T(8,128)(2,1)S(1)}, u32[]{:S(2)}, u32[]{:S(2)}) collective-permute-start(bf16[512,128]{1,0:T(8,128)(2,1)S(1)} %collective-permute-done.12), channel_id=1, source_target_pairs={{0,8},{8,16},{16,24},{24,0},{1,9},{9,17},{17,25},{25,1},{2,10},{10... | collective-permute-start | bytes 393224 | tf_op jit(solution)/shard_map/ppermute | solution.py:25
  88.6 52.0 %collective-permute-start.15 = (bf16[512,128]{1,0:T(8,128)(2,1)S(1)}, bf16[512,128]{1,0:T(8,128)(2,1)S(1)}, u32[]{:S(2)}, u32[]{:S(2)}) collective-permute-start(bf16[512,128]{1,0:T(8,128)(2,1)S(1)} %collective-permute-done.11), channel_id=1, source_target_pairs={{0,8},{8,16},{16,24},{24,0},{1,9},{9,17},{17,25},{25,1},{2,10},{10... | collective-permute-start | bytes 393224 | tf_op jit(solution)/shard_map/ppermute | solution.py:25
  91.4 50.7 %collective-permute-start.17 = (bf16[512,128]{1,0:T(8,128)(2,1)S(1)}, bf16[512,128]{1,0:T(8,128)(2,1)S(1)}, u32[]{:S(2)}, u32[]{:S(2)}) collective-permute-start(bf16[512,128]{1,0:T(8,128)(2,1)S(1)} %collective-permute-done.13), channel_id=1, source_target_pairs={{0,8},{8,16},{16,24},{24,0},{1,9},{9,17},{17,25},{25,1},{2,10},{10... | collective-permute-start | bytes 393224 | tf_op jit(solution)/shard_map/ppermute | solution.py:25
  93.4 15.2 %collective-permute-start = (bf16[512,3,128]{2,0,1:T(8,128)(2,1)}, bf16[512,3,128]{2,0,1:T(8,128)(2,1)}, u32[]{:S(2)}, u32[]{:S(2)}) collective-permute-start(bf16[512,3,128]{2,0,1:T(8,128)(2,1)} %copy.191), channel_id=1, source_target_pairs={{0,8},{8,0},{16,24},{24,16},{1,9},{9,1},{17,25},{25,17},{2,10},{10... | collective-permute-start | bytes 1179656 | tf_op jit(solution)/shard_map/ppermute | solution.py:19
  108.5 19.9 %collective-permute-start.1 = (bf16[512,3,128]{2,0,1:T(8,128)(2,1)}, bf16[512,3,128]{2,0,1:T(8,128)(2,1)S(1)}, u32[]{:S(2)}, u32[]{:S(2)}) collective-permute-start(bf16[512,3,128]{2,0,1:T(8,128)(2,1)} %collective-permute-done), channel_id=1, source_target_pairs={{0,16},{8,24},{16,0},{24,8},{1,17},{9,25},{17,1},{25,9},{2,18},{10... | collective-permute-start | bytes 1179656 | tf_op jit(solution)/shard_map/ppermute | solution.py:19
  145.7 9.1 %collective-permute-start.18 = (bf16[512,384]{0,1:T(8,128)(2,1)S(1)}, bf16[512,384]{0,1:T(8,128)(2,1)S(1)}, u32[]{:S(2)}, u32[]{:S(2)}) collective-permute-start(bf16[512,384]{0,1:T(8,128)(2,1)S(1)} %fusion.181), channel_id=1, source_target_pairs={{0,8},{8,0},{16,24},{24,16},{1,9},{9,1},{17,25},{25,17},{2,10},{10... | collective-permute-start | bytes 1179656 | tf_op jit(solution)/shard_map/ppermute | solution.py:19
  154.8 8.2 %collective-permute-start.19 = (bf16[512,384]{0,1:T(8,128)(2,1)S(1)}, bf16[512,384]{0,1:T(8,128)(2,1)S(1)}, u32[]{:S(2)}, u32[]{:S(2)}) collective-permute-start(bf16[512,384]{0,1:T(8,128)(2,1)S(1)} %collective-permute-done.18), channel_id=1, source_target_pairs={{0,16},{8,24},{16,0},{24,8},{1,17},{9,25},{17,1},{25,9},{2,18},{10... | collective-permute-start | bytes 1179656 | tf_op jit(solution)/shard_map/ppermute | solution.py:19
  247.2 42.1 %all-to-all-start.3 = ((bf16[8,128,768]{2,1,0:T(8,128)(2,1)}), bf16[8,128,768]{2,1,0:T(8,128)(2,1)}, u32[]{:S(2)}, u32[]{:S(2)}) async-start(bf16[8,128,768]{2,1,0:T(8,128)(2,1)} %fusion.223), calls=%async_computation.3 | async-start | bytes 3145728 | tf_op jit(solution)/shard_map/all_to_all | solution.py:237
  451.4 93.2 %all-to-all-start.5 = ((bf16[8,33,6144]{2,1,0:T(8,128)(2,1)}), bf16[8,33,6144]{2,1,0:T(8,128)(2,1)}, u32[]{:S(2)}, u32[]{:S(2)}) async-start(bf16[8,33,6144]{2,1,0:T(8,128)(2,1)} %reshape.493), calls=%async_computation.5 | async-start | bytes 7864320 | tf_op jit(solution)/shard_map/all_to_all | solution.py:288
  (20 other events, 131.5 us)
Sparse Core Ops, SparseCore 0:
  44.3 99.9 all-gather.4
  164.2 63.0 all-gather.2
